TPU v7x, 32 devices: a whole 2x2x4 slice. The times are simulated.
32 devices in a mesh: rep: 4 (over z), tp: 8 (over y, x, core).
Axes of the slice: x: 2, y: 2, z: 4, core: 2. Of those that a mesh axis runs over, the one named last changes fastest.
Arguments:
- exp_hidden: bfloat16 [256, 8192], P('rep', 'tp'), may hold values from -160 to 160
- exp_pre_gain: float32 [8192], P('tp'), may hold values from 0.25 to 1.75
- exp_gate: bfloat16 [8192, 28672], P('tp', 'rep'), may hold values from -0.0625 to 0.0625
- exp_up: bfloat16 [8192, 28672], P('tp', 'rep'), may hold values from -0.0625 to 0.0625
- exp_down: bfloat16 [28672, 8192], P('rep', 'tp'), may hold values from -0.03125 to 0.03125
- exp_out_gain: float32 [8192], P('tp'), may hold values from 0.25 to 1.75
- exp_head: bfloat16 [8192, 65536], P(None, ('rep', 'tp')), may hold values from -10 to 10
- ama_hidden: bfloat16 [256, 4096], P('rep', 'tp'), may hold values from -160 to 160
- ama_out_gain: float32 [4096], P('tp'), may hold values from 0.25 to 1.75
- ama_head: bfloat16 [4096, 65536], P(None, ('rep', 'tp')), may hold values from -10 to 10
- logit_scale: float32 [256], replicated, may hold values from 0.25 to 3
- prompt_of: int32 [256], replicated, may hold values from 0 to 7
- prior_picks: int32 [8, 24], replicated, may hold values from 0 to 65535
- valid_mask: int32 [65536], P(('rep', 'tp')), may hold values 0 or 1
Outputs:
- scores: float32 [256, 65536], P(None, ('rep', 'tp'))
- beam_best: float32 [256], replicated
All inputs are finite; a program needn't handle non-finite values. No bound on the sum of `valid_mask` on one device may be relied on, other than what follows from the above.
Results may differ from a plain program's by a relative error of at most 0.0034.
Values may be sent and summed in bfloat16 or wider, within the bound.
No kernel may reach another device: no remote copies, remote signals or barrier semaphores. Data moves between devices by JAX's collectives and lax.ppermute only.
A program may use at most 192 MiB of HBM per device.

v0:
```python
import jax
import jax.numpy as jnp
from jax import lax
from jax.sharding import PartitionSpec as P

DE = 8192
DA = 4096
norm_epsilon = 1e-05
contrast_weight = 0.5
hamming_weight = 0.7


def scaled_rows(values, squares, width, gain):
    return (values * lax.rsqrt(squares[:, None] / width + norm_epsilon) * gain).astype(jnp.bfloat16)


def both_halves(rows_in, gate_weight, up_weight):
    gate = jnp.dot(rows_in, gate_weight, preferred_element_type=jnp.float32)
    up = jnp.dot(rows_in, up_weight, preferred_element_type=jnp.float32)
    return jnp.concatenate([gate, up], axis=1)


def gated_rows(summed, width):
    return (jax.nn.silu(summed[:, :width]) * summed[:, width:]).astype(jnp.bfloat16)


def body(
    exp_hidden,
    exp_pre_gain,
    exp_gate,
    exp_up,
    exp_down,
    exp_out_gain,
    exp_head,
    ama_hidden,
    ama_out_gain,
    ama_head,
    logit_scale,
    prompt_of,
    prior_picks,
    valid_mask,
):
    values_exp = exp_hidden.astype(jnp.float32)
    values_ama = ama_hidden.astype(jnp.float32)
    squares_exp = lax.psum(jnp.sum(values_exp * values_exp, axis=1), "tp")
    normed_exp = scaled_rows(values_exp, squares_exp, DE, exp_pre_gain)
    rows_exp = lax.all_gather(normed_exp, "rep", axis=0, tiled=True)
    width_exp = exp_gate.shape[1]
    summed_exp = lax.psum_scatter(
        both_halves(rows_exp, exp_gate, exp_up), "tp", scatter_dimension=0, tiled=True
    )
    hidden_exp = gated_rows(summed_exp, width_exp)
    term_exp = jnp.dot(
        lax.all_gather(hidden_exp, "tp", axis=0, tiled=True),
        exp_down,
        preferred_element_type=jnp.float32,
    )
    out_exp = lax.psum_scatter(term_exp, "rep", scatter_dimension=0, tiled=True)
    layer_exp = values_exp + out_exp
    final_sq_exp, final_sq_ama = lax.psum(
        (jnp.sum(layer_exp * layer_exp, axis=1), jnp.sum(values_ama * values_ama, axis=1)), "tp"
    )
    final_exp = scaled_rows(layer_exp, final_sq_exp, DE, exp_out_gain)
    final_ama = scaled_rows(values_ama, final_sq_ama, DA, ama_out_gain)
    features_exp, features_ama = (
        lax.all_gather(final_exp, "tp", axis=1, tiled=True),
        lax.all_gather(final_ama, "tp", axis=1, tiled=True),
    )
    full_exp, full_ama = (
        lax.all_gather(features_exp, "rep", axis=0, tiled=True),
        lax.all_gather(features_ama, "rep", axis=0, tiled=True),
    )
    logits_exp = logit_scale[:, None] * jnp.dot(
        full_exp, exp_head, preferred_element_type=jnp.float32
    )
    logits_ama = logit_scale[:, None] * jnp.dot(
        full_ama, ama_head, preferred_element_type=jnp.float32
    )
    top_exp, top_ama = lax.pmax(
        (jnp.max(logits_exp, axis=1), jnp.max(logits_ama, axis=1)), ("rep", "tp")
    )
    local_exp = jnp.sum(jnp.exp(logits_exp - top_exp[:, None]), axis=1)
    local_ama = jnp.sum(jnp.exp(logits_ama - top_ama[:, None]), axis=1)
    total_exp, total_ama = lax.psum((local_exp, local_ama), ("rep", "tp"))
    logp_exp = logits_exp - top_exp[:, None] - jnp.log(total_exp)[:, None]
    logp_ama = logits_ama - top_ama[:, None] - jnp.log(total_ama)[:, None]
    entries = exp_head.shape[1]
    first_entry = lax.axis_index(("rep", "tp")) * entries
    vocab_ids = first_entry + jnp.arange(entries, dtype=jnp.int32)
    picks_row = jnp.take(prior_picks, prompt_of, axis=0)
    counts = jnp.sum(
        (picks_row[:, :, None] == vocab_ids[None, None, :]).astype(jnp.float32), axis=1
    )
    valid = valid_mask.astype(jnp.float32)[None, :]
    scores = logp_exp - contrast_weight * valid * logp_ama - hamming_weight * counts
    beam_best = lax.pmax(jnp.max(scores, axis=1), ("rep", "tp"))
    return (scores, beam_best)


def solution(mesh):
    placed = (
        P("rep", "tp"),
        P("tp"),
        P("tp", "rep"),
        P("tp", "rep"),
        P("rep", "tp"),
        P("tp"),
        P(None, ("rep", "tp")),
        P("rep", "tp"),
        P("tp"),
        P(None, ("rep", "tp")),
        P(),
        P(),
        P(),
        P(("rep", "tp")),
    )
    return jax.shard_map(
        body, mesh=mesh, in_specs=placed, out_specs=(P(None, ("rep", "tp")), P()), check_vma=False
    )
```

profile of v0, /device:TPU:0, one launch (start us, length us, event | category | flops | bytes accessed | tf_op | source)
XLA Modules:
  0.0 552.7 jit_solution(7237676692740054795)
XLA Ops:
  7.2 0.0 copy-start
  7.2 0.0 reduce-scatter.3.cloned.1.call-start
  7.2 1.0 fusion.1
  8.3 15.2 %psum.35 = f32[64]{0:T(128)S(1)} all-reduce(f32[64]{0:T(128)S(1)} %fusion.1), channel_id=1, replica_groups=mesh['rep'=4,'tp'=8] {'tp'}, use_global_device_ids=true, to_apply=%region_1.0 | all-reduce | flops 64 | bytes 512 | tf_op jit(solution)/shard_map/psum | solution.py:45
  23.4 1.0 fusion.3
  24.4 15.9 %all_gather.18 = bf16[256,1024]{1,0:T(8,128)(2,1)S(1)} all-gather(bf16[64,1024]{1,0:T(8,128)(2,1)S(1)} %fusion.3), channel_id=1, replica_groups=mesh['rep'=4,'tp'=8] {'rep'}, dimensions={0}, use_global_device_ids=true | all-gather | bytes 655360 | tf_op jit(solution)/shard_map/all_gather | solution.py:47
  40.4 0.0 copy-start.2
  40.4 7.4 %fusion.10 = f32[256,7168]{1,0:T(8,128)S(1)} fusion(bf16[256,1024]{1,0:T(8,128)(2,1)S(1)} %all_gather.18, bf16[1024,7168]{1,0:T(8,128)(2,1)} %param.16), kind=kOutput, calls=%fused_computation.35 | convolution fusion | flops 3758096384 | bytes 22544384 | tf_op jit(solution)/shard_map/dot_general | solution.py:18
  47.8 1.9 copy-done.2
  49.7 4.1 fusion.11
  53.8 5.5 pad_maximum_fusion
  59.3 0.0 reduce-scatter.3.cloned.1.call-update
  59.3 0.0 all-gather.5.cloned.1.call-start
  59.3 103.7 %reduce-scatter.3.cloned.1.call-done = f32[32,14336]{1,0:T(8,128)} async-done(((f32[256,14336]{1,0:T(8,128)}), f32[32,14336]{1,0:T(8,128)}) %reduce-scatter.3.cloned.1.call-update) | async-done | bytes 1835024 | tf_op jit(solution)/shard_map/reduce_scatter | solution.py:49
  163.1 2.5 fusion
  165.6 0.0 all-gather.5.cloned.1.call-update
  165.6 0.0 copy-start.4
  165.6 0.0 copy-start.3
  165.6 0.0 copy-start.6
  165.6 0.0 copy-start.7
  165.6 0.0 reduce-scatter.5.cloned.1.call-start
  165.7 34.4 %all-gather.5.cloned.1.call-done = bf16[256,7168]{1,0:T(8,128)(2,1)} async-done(((bf16[32,7168]{1,0:T(8,128)(2,1)}), bf16[256,7168]{1,0:T(8,128)(2,1)}) %all-gather.5.cloned.1.call-update) | async-done | bytes 3670032 | tf_op jit(solution)/shard_map/all_gather | solution.py:54
  200.1 11.2 %fusion.12 = f32[256,1024]{1,0:T(8,128)} fusion(bf16[256,7168]{1,0:T(8,128)(2,1)} %all-gather.5.cloned.1.call-done, bf16[7168,1024]{1,0:T(8,128)(2,1)} %param.18), kind=kOutput, calls=%fused_computation.37 | convolution fusion | flops 3758096384 | bytes 19398656 | tf_op jit(solution)/shard_map/dot_general | solution.py:53
  211.3 0.0 copy-start.8
  211.3 0.0 copy-start.5
  211.3 0.0 reduce-scatter.5.cloned.1.call-update
  211.4 0.0 copy-start.9
  211.4 0.0 all-gather.7.cloned.1.call-start
  211.4 0.0 copy-done.4
  211.4 0.1 fusion.4
  211.5 27.3 %reduce-scatter.5.cloned.1.call-done = f32[64,1024]{1,0:T(8,128)} async-done(((f32[256,1024]{1,0:T(8,128)}), f32[64,1024]{1,0:T(8,128)}) %reduce-scatter.5.cloned.1.call-update) | async-done | bytes 262160 | tf_op jit(solution)/shard_map/reduce_scatter | solution.py:58
  238.8 0.0 copy-done.3
  238.8 1.1 multiply_reduce_fusion
  239.9 13.2 %all-reduce.2 = (f32[64]{0:T(128)S(1)}, f32[64]{0:T(128)S(1)}) all-reduce(f32[64]{0:T(128)S(1)} %fusion.4, f32[64]{0:T(128)S(1)} %multiply_reduce_fusion), channel_id=1, replica_groups=mesh['rep'=4,'tp'=8] {'tp'}, use_global_device_ids=true, to_apply=%region_11.12 | all-reduce | flops 128 | bytes 1024 | tf_op jit(solution)/shard_map/psum | solution.py:60
  253.1 0.0 copy-done.6
  253.1 1.7 multiply_convert_fusion
  254.8 0.0 all-gather.7.cloned.1.call-update
  254.8 0.0 all-gather.11.cloned.1.call-start
  254.9 0.0 copy-done.7
  254.9 0.1 fusion.6
  255.0 10.5 %all_gather.22 = bf16[64,4096]{1,0:T(8,128)(2,1)} all-gather(bf16[64,512]{1,0:T(8,128)(2,1)S(1)} %fusion.6), channel_id=1, replica_groups=mesh['rep'=4,'tp'=8] {'tp'}, dimensions={1}, use_global_device_ids=true | all-gather | bytes 589824 | tf_op jit(solution)/shard_map/all_gather | solution.py:67
  265.5 0.0 all-gather.11.cloned.1.call-update
  265.6 0.2 all-gather.9.cloned.1.call-start
  265.8 9.6 %all-gather.7.cloned.1.call-done = bf16[64,8192]{1,0:T(8,128)(2,1)} async-done(((bf16[64,1024]{1,0:T(8,128)(2,1)}), bf16[64,8192]{1,0:T(8,128)(2,1)}) %all-gather.7.cloned.1.call-update) | async-done | bytes 1048592 | tf_op jit(solution)/shard_map/all_gather | solution.py:66
  275.4 0.0 all-gather.9.cloned.1.call-update
  275.4 0.0 copy-done.8
  275.5 0.0 copy-done
  275.5 0.7 gather_fusion
  276.2 0.0 copy-done.5
  276.3 0.1 broadcast_select_fusion
  276.4 20.6 %convert_reduce_fusion = f32[256,2048]{1,0:T(8,128)} fusion(s32[2048]{0:T(1024)S(1)} %iota_add_fusion, s32[256,24]{1,0:T(8,128)S(1)} %broadcast_select_fusion), kind=kLoop, calls=%fused_computation.1 | loop fusion | flops 37224448 | bytes 2129920 | tf_op jit(solution)/shard_map/reduce_sum | solution.py:91
  297.0 25.5 %all-gather.11.cloned.1.call-done = bf16[256,4096]{1,0:T(8,128)(2,1)} async-done(((bf16[64,4096]{1,0:T(8,128)(2,1)}), bf16[256,4096]{1,0:T(8,128)(2,1)}) %all-gather.11.cloned.1.call-update) | async-done | bytes 2097168 | tf_op jit(solution)/shard_map/all_gather | solution.py:71
  322.5 0.0 copy-done.9
  322.5 8.8 %fusion.8 = (f32[256]{0:T(256)S(1)}, f32[256,2048]{1,0:T(8,128)S(1)}) fusion(bf16[256,4096]{1,0:T(8,128)(2,1)} %all-gather.11.cloned.1.call-done, bf16[4096,2048]{1,0:T(8,128)(2,1)} %param.23, f32[256]{0:T(256)S(1)} %copy-done.9), kind=kOutput, calls=%fused_computation.33 | convolution fusion | flops 4296015872 | bytes 20973568 | tf_op jit(solution)/shard_map/dot_general | solution.py:76
  331.3 72.2 %all-gather.9.cloned.1.call-done = bf16[256,8192]{1,0:T(8,128)(2,1)} async-done(((bf16[64,8192]{1,0:T(8,128)(2,1)}), bf16[256,8192]{1,0:T(8,128)(2,1)}) %all-gather.9.cloned.1.call-update) | async-done | bytes 4194320 | tf_op jit(solution)/shard_map/all_gather | solution.py:70
  403.5 17.2 %fusion.9 = (f32[256]{0:T(256)S(1)}, f32[256,2048]{1,0:T(8,128)}) fusion(bf16[256,8192]{1,0:T(8,128)(2,1)} %all-gather.9.cloned.1.call-done, bf16[8192,2048]{1,0:T(8,128)(2,1)} %param.20, f32[256]{0:T(256)S(1)} %copy-done.9), kind=kOutput, calls=%fused_computation.34 | convolution fusion | flops 8590983168 | bytes 39847936 | tf_op jit(solution)/shard_map/dot_general | solution.py:73
  420.7 38.6 %all-reduce.1 = (f32[256]{0:T(256)S(1)}, f32[256]{0:T(256)S(1)}) all-reduce(f32[256]{0:T(256)S(1)} %get-tuple-element.10, f32[256]{0:T(256)S(1)} %get-tuple-element.12), channel_id=1, replica_groups=mesh['rep'=4,'tp'=8] {'rep','tp'}, use_global_device_ids=true, to_apply=%region_13.14 | all-reduce | flops 512 | bytes 4096 | tf_op jit(solution)/shard_map/pmax | solution.py:79
  459.4 2.3 exponential_reduce_fusion
  461.7 40.4 %all-reduce = (f32[256]{0:T(256)S(1)}, f32[256]{0:T(256)S(1)}) all-reduce(f32[256]{0:T(256)S(1)} %get-tuple-element.14, f32[256]{0:T(256)S(1)} %get-tuple-element.15), channel_id=1, replica_groups=mesh['rep'=4,'tp'=8] {'rep','tp'}, use_global_device_ids=true, to_apply=%region_15.16 | all-reduce | flops 512 | bytes 4096 | tf_op jit(solution)/shard_map/psum | solution.py:84
  502.1 0.0 copy-start.1
  502.1 4.4 fusion.7
  506.5 39.4 %pmax.23 = f32[256]{0:T(256)} all-reduce(f32[256]{0:T(256)S(1)} %get-tuple-element.8), channel_id=1, replica_groups=mesh['rep'=4,'tp'=8] {'rep','tp'}, use_global_device_ids=true, to_apply=%region_18.19 | all-reduce | flops 256 | bytes 2048 | tf_op jit(solution)/shard_map/pmax | solution.py:96
  545.9 0.0 copy-done.1
  (10 shorter events, 0.1 us)
Async XLA Ops:
  7.2 268.3 %copy-start = (s32[8,24]{1,0:T(8,128)S(1)}, s32[8,24]{1,0:T(8,128)}, u32[]{:S(2)}) copy-start(s32[8,24]{1,0:T(8,128)} %param.26) | copy-start | bytes 2308
  7.2 155.9 %reduce-scatter.3.cloned.1.call-start = ((), (), s32[]{:S(2)}) async-start(), calls=%async_computation.2 | async-start | bytes 16515072 | tf_op jit(solution)/shard_map/reduce_scatter | solution.py:49
  40.4 9.3 %copy-start.2 = (bf16[1024,7168]{1,0:T(8,128)(2,1)S(1)}, bf16[1024,7168]{1,0:T(8,128)(2,1)}, u32[]{:S(2)}) copy-start(bf16[1024,7168]{1,0:T(8,128)(2,1)} %param.17) | copy-start | bytes 44040196
  59.3 140.8 %all-gather.5.cloned.1.call-start = ((), (), s32[]{:S(2)}) async-start(), calls=%async_computation.3 | async-start | bytes 4128768 | tf_op jit(solution)/shard_map/all_gather | solution.py:54
  165.6 45.8 %copy-start.4 = (bf16[64,512]{1,0:T(8,128)(2,1)S(1)}, bf16[64,512]{1,0:T(8,128)(2,1)}, u32[]{:S(2)}) copy-start(bf16[64,512]{1,0:T(8,128)(2,1)} %param.21) | copy-start | bytes 196612
  165.6 73.2 %copy-start.3 = (bf16[64,1024]{1,0:T(8,128)(2,1)S(1)}, bf16[64,1024]{1,0:T(8,128)(2,1)}, u32[]{:S(2)}) copy-start(bf16[64,1024]{1,0:T(8,128)(2,1)} %param.14) | copy-start | bytes 393220
  165.6 87.5 %copy-start.6 = (f32[1024]{0:T(1024)S(1)}, f32[1024]{0:T(1024)}, u32[]{:S(2)}) copy-start(f32[1024]{0:T(1024)} %param.19) | copy-start | bytes 12292
  165.6 89.3 %copy-start.7 = (f32[512]{0:T(512)S(1)}, f32[512]{0:T(512)}, u32[]{:S(2)}) copy-start(f32[512]{0:T(512)} %param.22) | copy-start | bytes 6148
  165.6 73.2 %reduce-scatter.5.cloned.1.call-start = ((), (), s32[]{:S(2)}) async-start(), calls=%async_computation.4 | async-start | bytes 1310720 | tf_op jit(solution)/shard_map/reduce_scatter | solution.py:58
  211.3 64.1 %copy-start.8 = (s32[256]{0:T(256)S(1)}, s32[256]{0:T(256)}, u32[]{:S(2)}) copy-start(s32[256]{0:T(256)} %param.25) | copy-start | bytes 3076
  211.3 64.9 %copy-start.5 = (s32[2048]{0:T(1024)S(1)}, s32[2048]{0:T(1024)}, u32[]{:S(2)}) copy-start(s32[2048]{0:T(1024)} %param.27) | copy-start | bytes 24580
  211.4 111.2 %copy-start.9 = (f32[256]{0:T(256)S(1)}, f32[256]{0:T(256)}, u32[]{:S(2)}) copy-start(f32[256]{0:T(256)} %param.24) | copy-start | bytes 3076
  211.4 64.0 %all-gather.7.cloned.1.call-start = ((), (), s32[]{:S(2)}) async-start(), calls=%async_computation.5 | async-start | bytes 1179648 | tf_op jit(solution)/shard_map/all_gather | solution.py:66
  254.8 67.7 %all-gather.11.cloned.1.call-start = ((), (), s32[]{:S(2)}) async-start(), calls=%async_computation.7 | async-start | bytes 2621440 | tf_op jit(solution)/shard_map/all_gather | solution.py:71
  265.6 138.0 %all-gather.9.cloned.1.call-start = ((), (), s32[]{:S(2)}) async-start(), calls=%async_computation.6 | async-start | bytes 5242880 | tf_op jit(solution)/shard_map/all_gather | solution.py:70
  502.1 43.8 %copy-start.1 = (s32[8,24]{1,0:T(8,128)S(1)}, s32[8,24]{1,0:T(8,128)}, u32[]{:S(2)}) copy-start(s32[8,24]{1,0:T(8,128)} %param.26) | copy-start | bytes 2308
Sparse Core Ops, SparseCore 0:
  59.4 103.6 reduce-scatter.2
  165.7 34.3 all-gather.4
  211.5 27.2 reduce-scatter.4
  255.0 20.3 all-gather.6
  276.8 45.6 all-gather.10
  323.9 79.5 all-gather.8
where the time goes:
time: 553 us
  waiting for transfers between devices  273 us (49%)
  blocking collectives  173 us (31%)
  matrix products  48.7 us (9%)
  other arithmetic  40.4 us (7%)
  between operations  14.3 us (3%)
    reduce_scatter x1, waiting for transfers between devices, body(): lax.psum_scatter(both_halves(rows_exp, exp_gate, exp_up), 'tp', scatter_d...  104 us
    all_gather x1, waiting for transfers between devices, body(): lax.all_gather(features_exp, 'rep', axis=0, tiled=True)  72.2 us
    psum x1, blocking collectives, body(): total_exp, total_ama = lax.psum((local_exp, local_ama), ('rep', 'tp'))  40.4 us
    pmax x1, blocking collectives, body(): beam_best = lax.pmax(jnp.max(scores, axis=1), ('rep', 'tp'))  39.4 us
    pmax x1, blocking collectives, body(): lax.pmax((jnp.max(logits_exp, axis=1), jnp.max(logits_ama, axis=1)), ('re...  38.6 us
    all_gather x1, waiting for transfers between devices, body(): lax.all_gather(hidden_exp, 'tp', axis=0, tiled=True)  34.4 us
    reduce_scatter x1, waiting for transfers between devices, body(): out_exp = lax.psum_scatter(term_exp, 'rep', scatter_dimension=0, tiled=True)  27.3 us
    all_gather x1, waiting for transfers between devices, body(): lax.all_gather(features_ama, 'rep', axis=0, tiled=True)  25.5 us
  transfers between devices with their start and end apart: 6, of which 6 were waited for; matrix products, arithmetic and copies ran while one was open for 6% of the time, Pallas kernels for 0%

commit v1 on v0

--- a/solution.py
+++ b/solution.py
@@ -1,3 +1,4 @@
+import functools
 import jax
 import jax.numpy as jnp
 from jax import lax
@@ -8,6 +9,15 @@
 norm_epsilon = 1e-05
 contrast_weight = 0.5
 hamming_weight = 0.7
+
+
+def divide_chains(array_in, peer_axis, axis_key):
+    for tick in (peer_axis, axis_key):
+        array_in = jax.lax.psum(array_in, tick)
+    return array_in
+
+
+begin_row = functools.partial(divide_chains, peer_axis="tp", axis_key="rep")
 
 
 def scaled_rows(values, squares, width, gain):
@@ -81,7 +91,7 @@
     )
     local_exp = jnp.sum(jnp.exp(logits_exp - top_exp[:, None]), axis=1)
     local_ama = jnp.sum(jnp.exp(logits_ama - top_ama[:, None]), axis=1)
-    total_exp, total_ama = lax.psum((local_exp, local_ama), ("rep", "tp"))
+    total_exp, total_ama = begin_row((local_exp, local_ama))
     logp_exp = logits_exp - top_exp[:, None] - jnp.log(total_exp)[:, None]
     logp_ama = logits_ama - top_ama[:, None] - jnp.log(total_ama)[:, None]
     entries = exp_head.shape[1]

time: 553 us -> 534 us (0.966)
  blocking collectives: 173 us -> 154 us
    psum x1 -> x2, blocking collectives: 40.4 us -> 23.3 us  [divide_chains(): array_in = jax.lax.psum(array_in, tick)]
where the time goes in v1:
time: 534 us
  waiting for transfers between devices  273 us (51%)
  blocking collectives  154 us (29%)
  matrix products  48.7 us (9%)
  other arithmetic  40.4 us (8%)
  between operations  14.3 us (3%)
    reduce_scatter x1, waiting for transfers between devices, body(): lax.psum_scatter(both_halves(rows_exp, exp_gate, exp_up), 'tp', scatter_d...  104 us
    all_gather x1, waiting for transfers between devices, body(): lax.all_gather(features_exp, 'rep', axis=0, tiled=True)  72.2 us
    pmax x1, blocking collectives, body(): lax.pmax((jnp.max(logits_exp, axis=1), jnp.max(logits_ama, axis=1)), ('re...  38.6 us
    pmax x1, blocking collectives, body(): beam_best = lax.pmax(jnp.max(scores, axis=1), ('rep', 'tp'))  37.4 us
    all_gather x1, waiting for transfers between devices, body(): lax.all_gather(hidden_exp, 'tp', axis=0, tiled=True)  34.4 us
    reduce_scatter x1, waiting for transfers between devices, body(): out_exp = lax.psum_scatter(term_exp, 'rep', scatter_dimension=0, tiled=True)  27.3 us
    all_gather x1, waiting for transfers between devices, body(): lax.all_gather(features_ama, 'rep', axis=0, tiled=True)  25.5 us
    psum x2, blocking collectives, divide_chains(): array_in = jax.lax.psum(array_in, tick)  23.3 us
  transfers between devices with their start and end apart: 6, of which 6 were waited for; matrix products, arithmetic and copies ran while one was open for 6% of the time, Pallas kernels for 0%

profile of v1, /device:TPU:0, one launch (start us, length us, event | category | flops | bytes accessed | tf_op | source)
XLA Modules:
  0.0 533.6 jit_solution(4284419551679226307)
XLA Ops:
  7.2 0.0 copy-start
  7.2 0.0 reduce-scatter.3.cloned.1.call-start
  7.2 1.0 fusion.1
  8.3 15.2 %psum.49 = f32[64]{0:T(128)S(1)} all-reduce(f32[64]{0:T(128)S(1)} %fusion.1), channel_id=1, replica_groups=mesh['rep'=4,'tp'=8] {'tp'}, use_global_device_ids=true, to_apply=%region_1.0 | all-reduce | flops 64 | bytes 512 | tf_op jit(solution)/shard_map/psum | solution.py:55
  23.4 1.0 fusion.3
  24.4 15.9 %all_gather.18 = bf16[256,1024]{1,0:T(8,128)(2,1)S(1)} all-gather(bf16[64,1024]{1,0:T(8,128)(2,1)S(1)} %fusion.3), channel_id=1, replica_groups=mesh['rep'=4,'tp'=8] {'rep'}, dimensions={0}, use_global_device_ids=true | all-gather | bytes 655360 | tf_op jit(solution)/shard_map/all_gather | solution.py:57
  40.4 0.0 copy-start.2
  40.4 7.4 %fusion.10 = f32[256,7168]{1,0:T(8,128)S(1)} fusion(bf16[256,1024]{1,0:T(8,128)(2,1)S(1)} %all_gather.18, bf16[1024,7168]{1,0:T(8,128)(2,1)} %param.16), kind=kOutput, calls=%fused_computation.35 | convolution fusion | flops 3758096384 | bytes 22544384 | tf_op jit(solution)/shard_map/dot_general | solution.py:28
  47.8 1.9 copy-done.2
  49.7 4.1 fusion.11
  53.8 5.5 %pad_maximum_fusion = f32[256,14336]{1,0:T(8,128)} fusion(f32[256,7168]{1,0:T(8,128)S(1)} %fusion.11, f32[256,7168]{1,0:T(8,128)S(1)} %fusion.10), kind=kLoop, calls=%fused_computation.2 | loop fusion | flops 3670016 | bytes 29360128 | tf_op jit(solution)/shard_map/concatenate | solution.py:30
  59.3 0.0 reduce-scatter.3.cloned.1.call-update
  59.3 0.0 all-gather.5.cloned.1.call-start
  59.3 103.7 %reduce-scatter.3.cloned.1.call-done = f32[32,14336]{1,0:T(8,128)} async-done(((f32[256,14336]{1,0:T(8,128)}), f32[32,14336]{1,0:T(8,128)}) %reduce-scatter.3.cloned.1.call-update) | async-done | bytes 1835024 | tf_op jit(solution)/shard_map/reduce_scatter | solution.py:59
  163.1 2.5 fusion
  165.6 0.0 all-gather.5.cloned.1.call-update
  165.6 0.0 copy-start.4
  165.6 0.0 copy-start.3
  165.6 0.0 copy-start.6
  165.6 0.0 copy-start.7
  165.6 0.0 reduce-scatter.5.cloned.1.call-start
  165.7 34.4 %all-gather.5.cloned.1.call-done = bf16[256,7168]{1,0:T(8,128)(2,1)} async-done(((bf16[32,7168]{1,0:T(8,128)(2,1)}), bf16[256,7168]{1,0:T(8,128)(2,1)}) %all-gather.5.cloned.1.call-update) | async-done | bytes 3670032 | tf_op jit(solution)/shard_map/all_gather | solution.py:64
  200.1 11.2 %fusion.12 = f32[256,1024]{1,0:T(8,128)} fusion(bf16[256,7168]{1,0:T(8,128)(2,1)} %all-gather.5.cloned.1.call-done, bf16[7168,1024]{1,0:T(8,128)(2,1)} %param.18), kind=kOutput, calls=%fused_computation.37 | convolution fusion | flops 3758096384 | bytes 19398656 | tf_op jit(solution)/shard_map/dot_general | solution.py:63
  211.3 0.0 copy-start.8
  211.3 0.0 copy-start.5
  211.3 0.0 reduce-scatter.5.cloned.1.call-update
  211.4 0.0 copy-start.9
  211.4 0.0 all-gather.7.cloned.1.call-start
  211.4 0.0 copy-done.4
  211.4 0.1 fusion.4
  211.5 27.3 %reduce-scatter.5.cloned.1.call-done = f32[64,1024]{1,0:T(8,128)} async-done(((f32[256,1024]{1,0:T(8,128)}), f32[64,1024]{1,0:T(8,128)}) %reduce-scatter.5.cloned.1.call-update) | async-done | bytes 262160 | tf_op jit(solution)/shard_map/reduce_scatter | solution.py:68
  238.8 0.0 copy-done.3
  238.8 1.1 multiply_reduce_fusion
  239.9 13.2 %all-reduce.2 = (f32[64]{0:T(128)S(1)}, f32[64]{0:T(128)S(1)}) all-reduce(f32[64]{0:T(128)S(1)} %fusion.4, f32[64]{0:T(128)S(1)} %multiply_reduce_fusion), channel_id=1, replica_groups=mesh['rep'=4,'tp'=8] {'tp'}, use_global_device_ids=true, to_apply=%region_12.13 | all-reduce | flops 128 | bytes 1024 | tf_op jit(solution)/shard_map/psum | solution.py:70
  253.1 0.0 copy-done.6
  253.1 1.7 multiply_convert_fusion
  254.8 0.0 all-gather.7.cloned.1.call-update
  254.8 0.0 all-gather.11.cloned.1.call-start
  254.9 0.0 copy-done.7
  254.9 0.1 fusion.6
  255.0 10.5 %all_gather.22 = bf16[64,4096]{1,0:T(8,128)(2,1)} all-gather(bf16[64,512]{1,0:T(8,128)(2,1)S(1)} %fusion.6), channel_id=1, replica_groups=mesh['rep'=4,'tp'=8] {'tp'}, dimensions={1}, use_global_device_ids=true | all-gather | bytes 589824 | tf_op jit(solution)/shard_map/all_gather | solution.py:77
  265.5 0.0 all-gather.11.cloned.1.call-update
  265.6 0.2 all-gather.9.cloned.1.call-start
  265.8 9.6 %all-gather.7.cloned.1.call-done = bf16[64,8192]{1,0:T(8,128)(2,1)} async-done(((bf16[64,1024]{1,0:T(8,128)(2,1)}), bf16[64,8192]{1,0:T(8,128)(2,1)}) %all-gather.7.cloned.1.call-update) | async-done | bytes 1048592 | tf_op jit(solution)/shard_map/all_gather | solution.py:76
  275.4 0.0 all-gather.9.cloned.1.call-update
  275.4 0.0 copy-done.8
  275.5 0.0 copy-done
  275.5 0.7 gather_fusion
  276.2 0.0 copy-done.5
  276.3 0.1 broadcast_select_fusion
  276.4 20.6 %convert_reduce_fusion = f32[256,2048]{1,0:T(8,128)} fusion(s32[2048]{0:T(1024)S(1)} %iota_add_fusion, s32[256,24]{1,0:T(8,128)S(1)} %broadcast_select_fusion), kind=kLoop, calls=%fused_computation.1 | loop fusion | flops 37224448 | bytes 2129920 | tf_op jit(solution)/shard_map/reduce_sum | solution.py:101
  297.0 25.5 %all-gather.11.cloned.1.call-done = bf16[256,4096]{1,0:T(8,128)(2,1)} async-done(((bf16[64,4096]{1,0:T(8,128)(2,1)}), bf16[256,4096]{1,0:T(8,128)(2,1)}) %all-gather.11.cloned.1.call-update) | async-done | bytes 2097168 | tf_op jit(solution)/shard_map/all_gather | solution.py:81
  322.5 0.0 copy-done.9
  322.5 8.8 %fusion.8 = (f32[256]{0:T(256)S(1)}, f32[256,2048]{1,0:T(8,128)S(1)}) fusion(bf16[256,4096]{1,0:T(8,128)(2,1)} %all-gather.11.cloned.1.call-done, bf16[4096,2048]{1,0:T(8,128)(2,1)} %param.23, f32[256]{0:T(256)S(1)} %copy-done.9), kind=kOutput, calls=%fused_computation.33 | convolution fusion | flops 4296015872 | bytes 20973568 | tf_op jit(solution)/shard_map/dot_general | solution.py:86
  331.3 72.2 %all-gather.9.cloned.1.call-done = bf16[256,8192]{1,0:T(8,128)(2,1)} async-done(((bf16[64,8192]{1,0:T(8,128)(2,1)}), bf16[256,8192]{1,0:T(8,128)(2,1)}) %all-gather.9.cloned.1.call-update) | async-done | bytes 4194320 | tf_op jit(solution)/shard_map/all_gather | solution.py:80
  403.5 17.2 %fusion.9 = (f32[256]{0:T(256)S(1)}, f32[256,2048]{1,0:T(8,128)}) fusion(bf16[256,8192]{1,0:T(8,128)(2,1)} %all-gather.9.cloned.1.call-done, bf16[8192,2048]{1,0:T(8,128)(2,1)} %param.20, f32[256]{0:T(256)S(1)} %copy-done.9), kind=kOutput, calls=%fused_computation.34 | convolution fusion | flops 8590983168 | bytes 39847936 | tf_op jit(solution)/shard_map/dot_general | solution.py:83
  420.7 38.6 %all-reduce = (f32[256]{0:T(256)S(1)}, f32[256]{0:T(256)S(1)}) all-reduce(f32[256]{0:T(256)S(1)} %get-tuple-element.12, f32[256]{0:T(256)S(1)} %get-tuple-element.14), channel_id=1, replica_groups=mesh['rep'=4,'tp'=8] {'rep','tp'}, use_global_device_ids=true, to_apply=%region_14.15 | all-reduce | flops 512 | bytes 4096 | tf_op jit(solution)/shard_map/pmax | solution.py:89
  459.4 2.3 exponential_reduce_fusion
  461.7 12.7 %all-reduce.1 = (f32[256]{0:T(256)S(1)}, f32[256]{0:T(256)S(1)}) all-reduce(f32[256]{0:T(256)S(1)} %get-tuple-element.16, f32[256]{0:T(256)S(1)} %get-tuple-element.17), channel_id=1, replica_groups=mesh['rep'=4,'tp'=8] {'tp'}, use_global_device_ids=true, to_apply=%region_16.17 | all-reduce | flops 512 | bytes 4096 | tf_op jit(solution)/shard_map/psum | solution.py:16
  474.4 10.6 %all-reduce.3 = (f32[256]{0:T(256)S(1)}, f32[256]{0:T(256)S(1)}) all-reduce(f32[256]{0:T(256)S(1)} %get-tuple-element.4, f32[256]{0:T(256)S(1)} %get-tuple-element.5), channel_id=1, replica_groups=mesh['rep'=4,'tp'=8] {'rep'}, use_global_device_ids=true, to_apply=%region_17.18 | all-reduce | flops 512 | bytes 4096 | tf_op jit(solution)/shard_map/psum | solution.py:16
  485.0 0.0 copy-start.1
  485.0 4.4 fusion.7
  489.3 37.4 %pmax.23 = f32[256]{0:T(256)} all-reduce(f32[256]{0:T(256)S(1)} %get-tuple-element.10), channel_id=1, replica_groups=mesh['rep'=4,'tp'=8] {'rep','tp'}, use_global_device_ids=true, to_apply=%region_20.21 | all-reduce | flops 256 | bytes 2048 | tf_op jit(solution)/shard_map/pmax | solution.py:106
  526.8 0.0 copy-done.1
  (10 shorter events, 0.1 us)
Async XLA Ops:
  7.2 268.3 %copy-start = (s32[8,24]{1,0:T(8,128)S(1)}, s32[8,24]{1,0:T(8,128)}, u32[]{:S(2)}) copy-start(s32[8,24]{1,0:T(8,128)} %param.26) | copy-start | bytes 2308
  7.2 155.9 %reduce-scatter.3.cloned.1.call-start = ((), (), s32[]{:S(2)}) async-start(), calls=%async_computation.2 | async-start | bytes 16515072 | tf_op jit(solution)/shard_map/reduce_scatter | solution.py:59
  40.4 9.3 %copy-start.2 = (bf16[1024,7168]{1,0:T(8,128)(2,1)S(1)}, bf16[1024,7168]{1,0:T(8,128)(2,1)}, u32[]{:S(2)}) copy-start(bf16[1024,7168]{1,0:T(8,128)(2,1)} %param.17) | copy-start | bytes 44040196
  59.3 140.8 %all-gather.5.cloned.1.call-start = ((), (), s32[]{:S(2)}) async-start(), calls=%async_computation.3 | async-start | bytes 4128768 | tf_op jit(solution)/shard_map/all_gather | solution.py:64
  165.6 45.8 %copy-start.4 = (bf16[64,512]{1,0:T(8,128)(2,1)S(1)}, bf16[64,512]{1,0:T(8,128)(2,1)}, u32[]{:S(2)}) copy-start(bf16[64,512]{1,0:T(8,128)(2,1)} %param.21) | copy-start | bytes 196612
  165.6 73.2 %copy-start.3 = (bf16[64,1024]{1,0:T(8,128)(2,1)S(1)}, bf16[64,1024]{1,0:T(8,128)(2,1)}, u32[]{:S(2)}) copy-start(bf16[64,1024]{1,0:T(8,128)(2,1)} %param.14) | copy-start | bytes 393220
  165.6 87.5 %copy-start.6 = (f32[1024]{0:T(1024)S(1)}, f32[1024]{0:T(1024)}, u32[]{:S(2)}) copy-start(f32[1024]{0:T(1024)} %param.19) | copy-start | bytes 12292
  165.6 89.3 %copy-start.7 = (f32[512]{0:T(512)S(1)}, f32[512]{0:T(512)}, u32[]{:S(2)}) copy-start(f32[512]{0:T(512)} %param.22) | copy-start | bytes 6148
  165.6 73.2 %reduce-scatter.5.cloned.1.call-start = ((), (), s32[]{:S(2)}) async-start(), calls=%async_computation.4 | async-start | bytes 1310720 | tf_op jit(solution)/shard_map/reduce_scatter | solution.py:68
  211.3 64.1 %copy-start.8 = (s32[256]{0:T(256)S(1)}, s32[256]{0:T(256)}, u32[]{:S(2)}) copy-start(s32[256]{0:T(256)} %param.25) | copy-start | bytes 3076
  211.3 64.9 %copy-start.5 = (s32[2048]{0:T(1024)S(1)}, s32[2048]{0:T(1024)}, u32[]{:S(2)}) copy-start(s32[2048]{0:T(1024)} %param.27) | copy-start | bytes 24580
  211.4 111.2 %copy-start.9 = (f32[256]{0:T(256)S(1)}, f32[256]{0:T(256)}, u32[]{:S(2)}) copy-start(f32[256]{0:T(256)} %param.24) | copy-start | bytes 3076
  211.4 64.0 %all-gather.7.cloned.1.call-start = ((), (), s32[]{:S(2)}) async-start(), calls=%async_computation.5 | async-start | bytes 1179648 | tf_op jit(solution)/shard_map/all_gather | solution.py:76
  254.8 67.7 %all-gather.11.cloned.1.call-start = ((), (), s32[]{:S(2)}) async-start(), calls=%async_computation.7 | async-start | bytes 2621440 | tf_op jit(solution)/shard_map/all_gather | solution.py:81
  265.6 138.0 %all-gather.9.cloned.1.call-start = ((), (), s32[]{:S(2)}) async-start(), calls=%async_computation.6 | async-start | bytes 5242880 | tf_op jit(solution)/shard_map/all_gather | solution.py:80
  485.0 41.8 %copy-start.1 = (s32[8,24]{1,0:T(8,128)S(1)}, s32[8,24]{1,0:T(8,128)}, u32[]{:S(2)}) copy-start(s32[8,24]{1,0:T(8,128)} %param.26) | copy-start | bytes 2308
Sparse Core Ops, SparseCore 0:
  59.4 103.6 reduce-scatter.2
  165.7 34.3 all-gather.4
  211.5 27.2 reduce-scatter.4
  255.0 20.3 all-gather.6
  276.8 45.6 all-gather.10
  323.9 79.5 all-gather.8
